TPU v7x, 32 devices: a whole 2x2x4 slice. The times are simulated.
32 devices in a mesh: row: 2 (over x), col: 16 (over z, y, core).
Axes of the slice: x: 2, y: 2, z: 4, core: 2. Of those that a mesh axis runs over, the one named last changes fastest.
Arguments:
- upper_a: float32 [8, 2, 256, 16, 256], P(None, 'row', None, 'col'), may hold values from -0.375 to 0.375
- upper_b: float32 [8, 2, 256, 16, 256], P(None, 'row', None, 'col'), may hold values from -0.375 to 0.375
- right_side: float32 [8, 2, 256, 16, 256], P(None, 'row', None, 'col'), may hold values from -6 to 6
- vectors_a: float32 [8, 2, 256, 256], P(None, 'row'), may hold values from -0.375 to 0.375
- inverse_a: float32 [8, 2, 256, 256], P(None, 'row'), may hold values from -0.375 to 0.375
- values_a: float32 [8, 2, 256], P(None, 'row'), may hold values from 0.5 to 2
- vectors_b: float32 [16, 256, 256], P('col'), may hold values from -0.375 to 0.375
- inverse_b: float32 [16, 256, 256], P('col'), may hold values from -0.375 to 0.375
- values_b: float32 [16, 256], P('col'), may hold values from 0.5 to 2
Outputs:
- solved: float32 [8, 2, 256, 16, 256], P(None, 'row', None, 'col')
All inputs are finite; a program needn't handle non-finite values.
Results may differ from a plain program's by a relative error of at most 0.0001.
Values sent between devices are 32-bit elements; how exact they have to be, the bound alone decides.
A program may use at most 64 MiB of HBM per device.

v0:
```python
import jax
import jax.numpy as jnp
from jax import lax
from jax.sharding import PartitionSpec as P

FRONTS = 4
EXACT = lax.Precision.HIGHEST


def passed_along(value, axis, by):
    length = lax.axis_size(axis)
    pairs = [(i, i + by) for i in range(length) if 0 <= i + by < length]
    return lax.ppermute(value, axis, pairs)


def shifted(value, axis, steps):
    count = lax.axis_size(axis)
    pairs = [(source, (source + steps) % count) for source in range(count)]
    return lax.ppermute(value, axis, pairs)


def spread(value, axis, root):
    mine = lax.axis_index(axis) == root
    return lax.psum(jnp.where(mine, value, jnp.zeros_like(value)), axis)


def matmul(former, latter):
    return jnp.dot(former, latter, precision=EXACT, preferred_element_type=jnp.float32)


def diagonal_solve(residual, vectors_a, inverse_a, values_a, vectors_b, inverse_b, values_b):
    rotated = matmul(matmul(inverse_a, residual), vectors_b)
    scaled = rotated / (values_a[:, None] + values_b[None, :])
    return matmul(matmul(vectors_a, scaled), inverse_b)


def body(
    upper_a, upper_b, right_side, vectors_a, inverse_a, values_a, vectors_b, inverse_b, values_b
):
    row_count = lax.axis_size("row")
    col_count = lax.axis_size("col")
    row_pos = lax.axis_index("row")
    col_pos = lax.axis_index("col")
    local_blocks = right_side.shape[0]
    block_size = right_side.shape[2]
    square = (local_blocks, block_size, block_size)
    panel_a = upper_a.reshape(square)
    panel_b = upper_b.reshape(square)
    work = right_side.reshape(square)
    left_vectors = vectors_a.reshape(square)
    left_inverse = inverse_a.reshape(square)
    left_values = values_a.reshape(local_blocks, block_size)
    right_vectors = vectors_b.reshape(block_size, block_size)
    right_inverse = inverse_b.reshape(block_size, block_size)
    right_values = values_b.reshape(block_size)
    block_ids = jnp.arange(local_blocks, dtype=jnp.int32)
    global_rows = block_ids * row_count + row_pos
    offsets = list(range(-1, FRONTS - 1))
    moved_upper = {}
    for offset in offsets:
        if offset == 0:
            moved_upper[offset] = panel_a
        else:
            moved_upper[offset] = passed_along(panel_a, "col", offset)
    zero_block = jnp.zeros((1, block_size, block_size), jnp.float32)
    moved_lower = {}
    for offset in offsets:
        if offset % row_count == 0:
            arrived = panel_b
        else:
            arrived = shifted(panel_b, "row", -offset)
        block_carry = jnp.floor_divide(row_pos + offset, row_count)
        padded = jnp.concatenate([zero_block, arrived, zero_block], axis=0)
        moved_lower[offset] = lax.dynamic_slice_in_dim(padded, 1 + block_carry, local_blocks, 0)
    for offset in offsets:
        target = col_pos - offset
        slot_index = jnp.floor_divide(target - row_pos, row_count)
        present = (
            (jnp.remainder(target - row_pos, row_count) == 0) & (target >= 0) & (target < col_count)
        )
        picked = jnp.clip(slot_index, 0, local_blocks - 1)
        residual = lax.dynamic_index_in_dim(work, picked, 0, keepdims=False)
        solved = diagonal_solve(
            residual,
            lax.dynamic_index_in_dim(left_vectors, picked, 0, keepdims=False),
            lax.dynamic_index_in_dim(left_inverse, picked, 0, keepdims=False),
            lax.dynamic_index_in_dim(left_values, picked, 0, keepdims=False),
            right_vectors,
            right_inverse,
            right_values,
        )
        on_front = (block_ids == slot_index) & present
        work = jnp.where(on_front[:, None, None], solved[None], work)
        column_block = spread(solved, "row", jnp.remainder(target, row_count))
        upper_term = jnp.einsum("qab,bc->qac", moved_upper[offset], column_block, precision=EXACT)
        slot_blocks = jnp.where(on_front[:, None, None], solved[None], jnp.zeros_like(work))
        row_solved = lax.psum(slot_blocks, "col")
        lower_term = jnp.einsum("qab,qbc->qac", row_solved, moved_lower[offset], precision=EXACT)
        pending = col_pos - global_rows > offset
        work = jnp.where(pending[:, None, None], work - (upper_term + lower_term), work)
    return work.reshape(right_side.shape)


def solution(mesh):
    return jax.shard_map(
        body,
        mesh=mesh,
        in_specs=(
            P(None, "row", None, "col", None),
            P(None, "row", None, "col", None),
            P(None, "row", None, "col", None),
            P(None, "row", None, None),
            P(None, "row", None, None),
            P(None, "row", None),
            P("col", None, None),
            P("col", None, None),
            P("col", None),
        ),
        out_specs=P(None, "row", None, "col", None),
        check_vma=False,
    )
```

profile of v0, /device:TPU:0, one launch (start us, length us, event | category | flops | bytes accessed | tf_op | source)
XLA Modules:
  0.0 592.5 jit_solution(1330975827765755095)
XLA Ops:
  6.5 3.2 copy.54
  9.7 3.0 collective-permute-start.1
  12.7 1.5 copy.55
  14.3 1.4 collective-permute-start
  15.8 1.1 constant_dynamic-slice_fusion.4
  17.0 0.4 fusion.13
  17.4 0.4 convolution_divide_fusion.3
  17.8 1.3 fusion.41
  19.1 1.1 broadcast_select_fusion.7
  20.5 1.7 broadcast_select_fusion.3
  22.5 6.0 %copy.11 = f32[8,1,256,1,256]{2,4,0,3,1:T(8,128)} copy(f32[8,1,256,1,256]{4,3,2,1,0:T(1,128)} %param.11) | data formatting | bytes 4194304 | tf_op args[2]
  28.6 35.7 %collective-permute-done.1 = f32[8,256,256]{2,1,0:T(8,128)} collective-permute-done((f32[8,256,256]{2,1,0:T(8,128)}, f32[8,256,256]{2,1,0:T(8,128)}, u32[]{:S(2)}, u32[]{:S(2)}) %collective-permute-start.1) | collective-permute-done | bytes 2097184 | tf_op jit(solution)/shard_map/ppermute | solution.py:19
  64.3 5.4 pad_maximum_fusion
  69.7 6.5 %fusion.26 = f32[256,8,256]{2,0,1:T(8,128)} fusion(f32[8,256,256]{2,1,0:T(8,128)} %collective-permute-done, f32[256,256]{1,0:T(8,128)} %all-reduce.9.cloned.1.call-done), kind=kOutput, calls=%fused_computation.45 | convolution fusion | flops 1610612736 | bytes 4456448 | tf_op jit(solution)/shard_map/qab,bc->qac/dot_general | solution.py:95
  76.2 77.0 %all-reduce.11.cloned.1.call-done = f32[8,256,256]{1,2,0:T(8,128)} async-done(((f32[8,256,256]{1,2,0:T(8,128)}), f32[8,256,256]{1,2,0:T(8,128)}) %all-reduce.11.cloned.1.call-update) | async-done | bytes 2097168 | tf_op jit(solution)/shard_map/psum | solution.py:97
  153.2 7.2 %subtract_select_fusion.3 = f32[8,256,256]{1,2,0:T(8,128)S(1)} fusion(f32[256,8,256]{2,0,1:T(8,128)} %fusion.26, f32[8,1,256,1,256]{2,4,0,3,1:T(8,128)} %copy.11, f32[8,256,256]{1,2,0:T(8,128)} %all-reduce.11.cloned.1.call-done, f32[10,256,256]{2,1,0:T(8,128)} %get-tuple-element.8, s32[]{:T(128)S(6)} %select_n.168, f32[256,256]{0,1:T(8,128)S(1)} %copy.10, ...), kind=kOutput, calls=%fused_computation.7 | convolution fusion | flops 1612709888 | bytes 10747924 | tf_op jit(solution)/shard_map/qab,qbc->qac/dot_general | solution.py:98
  160.4 1.3 copy-done.2
  161.7 0.4 fusion.24
  162.5 1.3 fusion.44
  163.9 1.1 broadcast_select_fusion.6
  165.1 1.7 broadcast_select_fusion.2
  166.9 2.7 collective-permute-start.2
  169.6 0.6 all-reduce.17.cloned.1.call-start
  170.2 98.3 %all-reduce.15.cloned.1.call-done = f32[8,256,256]{1,2,0:T(8,128)} async-done(((f32[8,256,256]{1,2,0:T(8,128)}), f32[8,256,256]{1,2,0:T(8,128)}) %all-reduce.15.cloned.1.call-update) | async-done | bytes 2097168 | tf_op jit(solution)/shard_map/psum | solution.py:97
  268.5 7.2 %fusion.5 = f32[8,256,256]{1,2,0:T(8,128)} fusion(f32[8,256,256]{1,2,0:T(8,128)} %all-reduce.15.cloned.1.call-done, f32[10,256,256]{2,1,0:T(8,128)} %get-tuple-element.7, s32[]{:T(128)S(6)} %select_n.176), kind=kOutput, calls=%fused_computation.20 | convolution fusion | flops 1610612736 | bytes 6291460 | tf_op jit(solution)/shard_map/qab,qbc->qac/dot_general | solution.py:98
  275.7 17.7 %all-reduce.13.cloned.1.call-done = f32[256,256]{1,0:T(8,128)} async-done(((f32[256,256]{1,0:T(8,128)}), f32[256,256]{1,0:T(8,128)}) %all-reduce.13.cloned.1.call-update) | async-done | bytes 262160 | tf_op jit(solution)/shard_map/psum | solution.py:24
  293.4 6.7 %subtract_select_fusion.2 = f32[8,256,256]{1,2,0:T(8,128)S(1)} fusion(f32[8,256,256]{1,2,0:T(8,128)} %fusion.5, f32[8,256,256]{1,2,0:T(8,128)} %copy-done.2, f32[256,256]{0,1:T(8,128)S(1)} %copy.15, pred[8]{0:T(512)(128)(4,1)S(1)} %compare_and_fusion.1, pred[8]{0:T(512)(128)(4,1)S(1)} %get-tuple-element.14, f32[256,256]{1,0:T(8,128)} %all-reduce.13.cloned.1.call-done, ...), kind=kOutput, calls=%fused_computation.6 | convolution fusion | flops 1612709888 | bytes 8912912 | tf_op jit(solution)/shard_map/qab,bc->qac/dot_general | solution.py:95
  300.2 1.3 copy-done.1
  301.4 0.4 fusion.21
  302.3 1.3 fusion.47
  303.6 1.1 broadcast_select_fusion.5
  304.9 1.6 broadcast_select_fusion.1
  306.5 4.9 collective-permute-start.3
  311.5 16.8 %all-reduce.17.cloned.1.call-done = f32[256,256]{1,0:T(8,128)} async-done(((f32[256,256]{1,0:T(8,128)}), f32[256,256]{1,0:T(8,128)}) %all-reduce.17.cloned.1.call-update) | async-done | bytes 262160 | tf_op jit(solution)/shard_map/psum | solution.py:24
  328.3 6.5 %fusion.19 = f32[256,8,256]{2,0,1:T(8,128)} fusion(f32[8,256,256]{2,1,0:T(8,128)} %collective-permute-done.2, f32[256,256]{1,0:T(8,128)} %all-reduce.17.cloned.1.call-done), kind=kOutput, calls=%fused_computation.38 | convolution fusion | flops 1610612736 | bytes 4456448 | tf_op jit(solution)/shard_map/qab,bc->qac/dot_general | solution.py:95
  334.8 100.3 %all-reduce.19.cloned.1.call-done = f32[8,256,256]{1,2,0:T(8,128)} async-done(((f32[8,256,256]{1,2,0:T(8,128)}), f32[8,256,256]{1,2,0:T(8,128)}) %all-reduce.19.cloned.1.call-update) | async-done | bytes 2097168 | tf_op jit(solution)/shard_map/psum | solution.py:97
  435.1 7.2 %subtract_select_fusion.1 = f32[8,256,256]{1,2,0:T(8,128)S(1)} fusion(f32[256,8,256]{2,0,1:T(8,128)} %fusion.19, f32[8,256,256]{1,2,0:T(8,128)} %copy-done.1, f32[8,256,256]{1,2,0:T(8,128)} %all-reduce.19.cloned.1.call-done, f32[10,256,256]{2,1,0:T(8,128)} %get-tuple-element.8, s32[]{:T(128)S(6)} %select_n.184, f32[256,256]{0,1:T(8,128)S(1)} %copy.19, ...), kind=kOutput, calls=%fused_computation.5 | convolution fusion | flops 1612709888 | bytes 10747924 | tf_op jit(solution)/shard_map/qab,qbc->qac/dot_general | solution.py:98
  442.3 1.3 copy-done.3
  443.7 0.4 fusion.17
  444.5 1.3 fusion.50
  445.8 1.1 broadcast_select_fusion.4
  447.0 1.5 broadcast_select_fusion
  448.9 0.5 all-reduce.21.cloned.1.call-update
  449.3 97.0 %all-reduce.23.cloned.1.call-done = f32[8,256,256]{1,2,0:T(8,128)} async-done(((f32[8,256,256]{1,2,0:T(8,128)}), f32[8,256,256]{1,2,0:T(8,128)}) %all-reduce.23.cloned.1.call-update) | async-done | bytes 2097168 | tf_op jit(solution)/shard_map/psum | solution.py:97
  546.4 7.0 %fusion.1 = f32[8,256,256]{1,2,0:T(8,128)} fusion(f32[8,256,256]{1,2,0:T(8,128)} %all-reduce.23.cloned.1.call-done, f32[10,256,256]{2,1,0:T(8,128)} %get-tuple-element.7, s32[]{:T(128)S(6)} %select_n.192), kind=kOutput, calls=%fused_computation.16 | convolution fusion | flops 1610612736 | bytes 6291460 | tf_op jit(solution)/shard_map/qab,qbc->qac/dot_general | solution.py:98
  553.4 18.0 %all-reduce.21.cloned.1.call-done = f32[256,256]{1,0:T(8,128)} async-done(((f32[256,256]{1,0:T(8,128)}), f32[256,256]{1,0:T(8,128)}) %all-reduce.21.cloned.1.call-update) | async-done | bytes 262160 | tf_op jit(solution)/shard_map/psum | solution.py:24
  571.5 8.0 %fusion = f32[8,1,256,1,256]{2,4,0,3,1:T(8,128)} fusion(f32[8,256,256]{1,2,0:T(8,128)} %fusion.1, f32[8,256,256]{1,2,0:T(8,128)} %copy-done.3, f32[8,256,256]{2,1,0:T(8,128)} %collective-permute-done.3, f32[256,256]{0,1:T(8,128)S(1)} %copy.23, pred[8]{0:T(512)(128)(4,1)S(1)} %compare_and_fusion.3, pred[8]{0:T(512)(128)(4,1)S(1)} %get-tuple-element.5, ...), kind=kOutput, calls=%fused_computation.8 | convolution fusion | flops 1612709888 | bytes 8912912 | tf_op jit(solution)/shard_map/qab,bc->qac/dot_general | solution.py:95
  579.4 6.0 %copy.27 = f32[8,1,256,1,256]{4,3,2,1,0:T(1,128)} copy(f32[8,1,256,1,256]{2,4,0,3,1:T(8,128)} %fusion) | data formatting | bytes 4194304 | tf_op jit(solution)/shard_map/reshape | solution.py:101
  (48 shorter events, 2.6 us)
Async XLA Ops:
  6.5 10.4 %copy-start = (f32[8,1,256,256]{3,2,1,0:T(8,128)S(1)}, f32[8,1,256,256]{3,2,1,0:T(8,128)}, u32[]{:S(2)}) copy-start(f32[8,1,256,256]{3,2,1,0:T(8,128)} %param.13) | copy-start | bytes 6291460
  6.5 63.1 %all-reduce.9.cloned.1.call-start = ((), (), s32[]{:S(2)}) async-start(), calls=%async_computation | async-start | bytes 524288 | tf_op jit(solution)/shard_map/psum | solution.py:24
  6.5 6.2 %copy-start.4 = (f32[8,1,256,1,256]{4,3,2,1,0:T(1,128)S(1)}, f32[8,1,256,1,256]{4,3,2,1,0:T(1,128)}, u32[]{:S(2)}) copy-start(f32[8,1,256,1,256]{4,3,2,1,0:T(1,128)} %param.9) | copy-start | bytes 6291460
  9.7 7.2 %copy-start.6 = (f32[8,1,256]{2,1,0:T(1,128)S(1)}, f32[8,1,256]{2,1,0:T(1,128)}, u32[]{:S(2)}) copy-start(f32[8,1,256]{2,1,0:T(1,128)} %param.14) | copy-start | bytes 24580
  9.7 7.6 %copy-start.7 = (f32[1,256,256]{2,1,0:T(8,128)S(1)}, f32[1,256,256]{2,1,0:T(8,128)}, u32[]{:S(2)}) copy-start(f32[1,256,256]{2,1,0:T(8,128)} %param.15) | copy-start | bytes 786436
  9.7 7.7 %copy-start.8 = (f32[1,256]{1,0:T(1,128)S(1)}, f32[1,256]{1,0:T(1,128)}, u32[]{:S(2)}) copy-start(f32[1,256]{1,0:T(1,128)} %param.17) | copy-start | bytes 3076
  9.7 54.5 %collective-permute-start.1 = (f32[8,256,256]{2,1,0:T(8,128)}, f32[8,256,256]{2,1,0:T(8,128)}, u32[]{:S(2)}, u32[]{:S(2)}) collective-permute-start(f32[8,256,256]{2,1,0:T(8,128)} %bitcast.125), channel_id=1, source_target_pairs={{0,16},{16,0},{1,17},{17,1},{2,18},{18,2},{3,19},{19,3},{4,20},{20... | collective-permute-start | bytes 6291464 | tf_op jit(solution)/shard_map/ppermute | solution.py:19
  14.3 4.9 copy-start.5
  14.3 55.4 %collective-permute-start = (f32[8,256,256]{2,1,0:T(8,128)}, f32[8,256,256]{2,1,0:T(8,128)}, u32[]{:S(2)}, u32[]{:S(2)}) collective-permute-start(f32[8,256,256]{2,1,0:T(8,128)} %bitcast.126), channel_id=1, source_target_pairs={{1,0},{2,1},{3,2},{4,3},{5,4},{6,5},{7,6},{8,7},{9,8},{10,9},{11,1... | collective-permute-start | bytes 6291464 | tf_op jit(solution)/shard_map/ppermute | solution.py:13
  20.2 132.9 %all-reduce.11.cloned.1.call-start = ((), (), s32[]{:S(2)}) async-start(), calls=%async_computation.1 | async-start | bytes 4194304 | tf_op jit(solution)/shard_map/psum | solution.py:97
  22.2 246.3 %all-reduce.15.cloned.1.call-start = ((), (), s32[]{:S(2)}) async-start(), calls=%async_computation.3 | async-start | bytes 4194304 | tf_op jit(solution)/shard_map/psum | solution.py:97
  160.4 1.4 copy-start.2
  166.8 126.6 %all-reduce.13.cloned.1.call-start = ((), (), s32[]{:S(2)}) async-start(), calls=%async_computation.2 | async-start | bytes 524288 | tf_op jit(solution)/shard_map/psum | solution.py:24
  166.9 144.6 %collective-permute-start.2 = (f32[8,256,256]{2,1,0:T(8,128)}, f32[8,256,256]{2,1,0:T(8,128)}, u32[]{:S(2)}, u32[]{:S(2)}) collective-permute-start(f32[8,256,256]{2,1,0:T(8,128)} %bitcast.126), channel_id=1, source_target_pairs={{0,1},{1,2},{2,3},{3,4},{4,5},{5,6},{6,7},{7,8},{8,9},{9,10},{10,1... | collective-permute-start | bytes 6291464 | tf_op jit(solution)/shard_map/ppermute | solution.py:13
  169.6 158.7 %all-reduce.17.cloned.1.call-start = ((), (), s32[]{:S(2)}) async-start(), calls=%async_computation.4 | async-start | bytes 524288 | tf_op jit(solution)/shard_map/psum | solution.py:24
  300.1 1.3 copy-start.1
  304.8 130.2 %all-reduce.19.cloned.1.call-start = ((), (), s32[]{:S(2)}) async-start(), calls=%async_computation.5 | async-start | bytes 4194304 | tf_op jit(solution)/shard_map/psum | solution.py:97
  306.5 239.9 %all-reduce.23.cloned.1.call-start = ((), (), s32[]{:S(2)}) async-start(), calls=%async_computation.7 | async-start | bytes 4194304 | tf_op jit(solution)/shard_map/psum | solution.py:97
  306.5 246.9 %collective-permute-start.3 = (f32[8,256,256]{2,1,0:T(8,128)}, f32[8,256,256]{2,1,0:T(8,128)}, u32[]{:S(2)}, u32[]{:S(2)}) collective-permute-start(f32[8,256,256]{2,1,0:T(8,128)} %bitcast.126), channel_id=1, source_target_pairs={{0,2},{1,3},{2,4},{3,5},{4,6},{5,7},{6,8},{7,9},{8,10},{9,11},{10,... | collective-permute-start | bytes 6291464 | tf_op jit(solution)/shard_map/ppermute | solution.py:13
  442.3 1.4 copy-start.3
  448.6 122.9 %all-reduce.21.cloned.1.call-start = ((), (), s32[]{:S(2)}) async-start(), calls=%async_computation.6 | async-start | bytes 524288 | tf_op jit(solution)/shard_map/psum | solution.py:24
Sparse Core Ops, SparseCore 0:
  20.4 31.0 all-reduce.8
  55.0 98.1 all-reduce.10
  166.9 101.5 all-reduce.14
  270.6 22.7 all-reduce.12
  305.0 23.2 all-reduce.16
  331.7 103.3 all-reduce.18
  448.7 97.6 all-reduce.22
  548.7 22.7 all-reduce.20
where the time goes:
time: 596 us; the launch traced here: 592 us
  waiting for transfers between devices  462 us (78%)
  matrix products  69 us (12%)
  local copies, waits for them, and re-layouts  22.5 us (4%)
  between operations  14.2 us (2%)
  starting transfers between devices  13.3 us (2%)
  other arithmetic  11.9 us (2%)
    psum x4, waiting for transfers between devices, body(): row_solved = lax.psum(slot_blocks, 'col')  373 us
    psum x4, waiting for transfers between devices, spread(): return lax.psum(jnp.where(mine, value, jnp.zeros_like(value)), axis)  52.6 us
    ppermute x1, waiting for transfers between devices, shifted(): return lax.ppermute(value, axis, pairs)  35.7 us
    dot_general x4, matrix products, body(): jnp.einsum('qab,qbc->qac', row_solved, moved_lower[offset], precision=EXACT)  28.6 us
    dot_general x4, matrix products, body(): jnp.einsum('qab,bc->qac', moved_upper[offset], column_block, precision=EX...  27.6 us
    unnamed x21, local copies, waits for them, and re-layouts  14.8 us
    dot_general x16, matrix products, matmul(): jnp.dot(former, latter, precision=EXACT, preferred_element_type=jnp.float32)  12.8 us
  transfers between devices with their start and end apart: 12, of which 8 were waited for; matrix products, arithmetic and copies ran while one was open for 12% of the time, Pallas kernels for 0%

commit v1 on v0

--- a/solution.py
+++ b/solution.py
@@ -5,6 +5,14 @@
 
 FRONTS = 4
 EXACT = lax.Precision.HIGHEST
+
+
+def doubling_sum(x, axis):
+    size, total = (lax.axis_size(axis), x)
+    for far in [1 << k for k in range(size.bit_length() - 1)]:
+        swap = [(i, i ^ far) for i in range(size)]
+        total = total + lax.ppermute(total, axis, swap)
+    return total
 
 
 def passed_along(value, axis, by):
@@ -94,7 +102,7 @@
         column_block = spread(solved, "row", jnp.remainder(target, row_count))
         upper_term = jnp.einsum("qab,bc->qac", moved_upper[offset], column_block, precision=EXACT)
         slot_blocks = jnp.where(on_front[:, None, None], solved[None], jnp.zeros_like(work))
-        row_solved = lax.psum(slot_blocks, "col")
+        row_solved = doubling_sum(slot_blocks, "col")
         lower_term = jnp.einsum("qab,qbc->qac", row_solved, moved_lower[offset], precision=EXACT)
         pending = col_pos - global_rows > offset
         work = jnp.where(pending[:, None, None], work - (upper_term + lower_term), work)

time: 596 us -> 849 us (1.42)
  waiting for transfers between devices: 462 us -> 699 us
  starting transfers between devices: 13.3 us -> 30.4 us
    ppermute x0 -> x16, waiting for transfers between devices: none -> 617 us  [doubling_sum(): total = total + lax.ppermute(total, axis, swap)]
    psum x4 -> x0, waiting for transfers between devices: 373 us -> none  [body(): row_solved = lax.psum(slot_blocks, 'col')]
    ppermute x1, waiting for transfers between devices: 35.7 us -> 0.01 us  [shifted(): return lax.ppermute(value, axis, pairs)]
    psum x4, waiting for transfers between devices: 52.6 us -> 81.8 us  [spread(): return lax.psum(jnp.where(mine, value, jnp.zeros_like(value)), axis)]
    ppermute x0 -> x16, starting transfers between devices: none -> 18.9 us  [doubling_sum(): total = total + lax.ppermute(total, axis, swap)]
    add x0 -> x12, other arithmetic: none -> 9.12 us  [doubling_sum(): total = total + lax.ppermute(total, axis, swap)]
  transfers between devices with their start and end apart: 12 -> 24, of which waited for: 8 -> 20; matrix products, arithmetic and copies ran while one was open for 12% -> 5% of each run, Pallas kernels for 0% -> 0%
where the time goes in v1:
time: 849 us; the launch traced here: 845 us
  waiting for transfers between devices  699 us (82%)
  matrix products  63.9 us (8%)
  starting transfers between devices  30.4 us (4%)
  local copies, waits for them, and re-layouts  22.2 us (3%)
  other arithmetic  15.4 us (2%)
  between operations  14 us (2%)
    ppermute x16, waiting for transfers between devices, doubling_sum(): total = total + lax.ppermute(total, axis, swap)  617 us
    psum x4, waiting for transfers between devices, spread(): return lax.psum(jnp.where(mine, value, jnp.zeros_like(value)), axis)  81.8 us
    dot_general x4, matrix products, body(): jnp.einsum('qab,qbc->qac', row_solved, moved_lower[offset], precision=EXACT)  28.9 us
    dot_general x4, matrix products, body(): jnp.einsum('qab,bc->qac', moved_upper[offset], column_block, precision=EX...  21.2 us
    ppermute x16, starting transfers between devices, doubling_sum(): total = total + lax.ppermute(total, axis, swap)  18.9 us
  transfers between devices with their start and end apart: 24, of which 20 were waited for; matrix products, arithmetic and copies ran while one was open for 5% of the time, Pallas kernels for 0%

profile of v1, /device:TPU:0, one launch (start us, length us, event | category | flops | bytes accessed | tf_op | source)
XLA Modules:
  0.0 845.1 jit_solution(7122548077572016746)
XLA Ops:
  14.1 3.8 collective-permute-done.1
  18.2 2.9 collective-permute-start.2
  21.2 45.9 %collective-permute-done.2 = f32[8,256,256]{1,2,0:T(8,128)S(1)} collective-permute-done((f32[8,256,256]{1,2,0:T(8,128)S(1)}, f32[8,256,256]{1,2,0:T(8,128)S(1)}, u32[]{:S(2)}, u32[]{:S(2)}) %collective-permute-start.2) | collective-permute-done | bytes 2097184 | tf_op jit(solution)/shard_map/ppermute | solution.py:14
  67.5 1.9 collective-permute-start.3
  69.3 1.6 copy.54
  70.9 1.5 collective-permute-start.5
  72.4 1.5 copy.55
  75.2 39.4 %collective-permute-done.3 = f32[8,256,256]{1,2,0:T(8,128)S(1)} collective-permute-done((f32[8,256,256]{1,2,0:T(8,128)S(1)}, f32[8,256,256]{1,2,0:T(8,128)S(1)}, u32[]{:S(2)}, u32[]{:S(2)}) %collective-permute-start.3) | collective-permute-done | bytes 2097184 | tf_op jit(solution)/shard_map/ppermute | solution.py:14
  114.6 1.6 add.252
  116.2 2.5 collective-permute-start.4
  119.2 6.1 copy.11
  125.3 5.3 pad_maximum_fusion
  130.5 10.9 %all-reduce.5.cloned.1.call-done = f32[256,256]{1,0:T(8,128)} async-done(((f32[256,256]{1,0:T(8,128)}), f32[256,256]{1,0:T(8,128)}) %all-reduce.5.cloned.1.call-update) | async-done | bytes 262160 | tf_op jit(solution)/shard_map/psum | solution.py:32
  141.4 5.3 fusion.36
  146.8 62.0 %collective-permute-done.4 = f32[8,256,256]{1,2,0:T(8,128)} collective-permute-done((f32[8,256,256]{1,2,0:T(8,128)}, f32[8,256,256]{1,2,0:T(8,128)}, u32[]{:S(2)}, u32[]{:S(2)}) %collective-permute-start.4) | collective-permute-done | bytes 2097184 | tf_op jit(solution)/shard_map/ppermute | solution.py:14
  208.7 6.9 subtract_select_fusion.3
  220.7 4.1 collective-permute-done.6
  226.4 46.5 %collective-permute-done.7 = f32[8,256,256]{1,2,0:T(8,128)S(1)} collective-permute-done((f32[8,256,256]{1,2,0:T(8,128)S(1)}, f32[8,256,256]{1,2,0:T(8,128)S(1)}, u32[]{:S(2)}, u32[]{:S(2)}) %collective-permute-start.7) | collective-permute-done | bytes 2097184 | tf_op jit(solution)/shard_map/ppermute | solution.py:14
  273.6 46.5 %collective-permute-done.8 = f32[8,256,256]{1,2,0:T(8,128)S(1)} collective-permute-done((f32[8,256,256]{1,2,0:T(8,128)S(1)}, f32[8,256,256]{1,2,0:T(8,128)S(1)}, u32[]{:S(2)}, u32[]{:S(2)}) %collective-permute-start.8) | collective-permute-done | bytes 2097184 | tf_op jit(solution)/shard_map/ppermute | solution.py:14
  320.1 1.7 add.264
  321.8 2.0 collective-permute-start.9
  324.4 22.2 %all-reduce.7.cloned.1.call-done = f32[256,256]{1,0:T(8,128)} async-done(((f32[256,256]{1,0:T(8,128)}), f32[256,256]{1,0:T(8,128)}) %all-reduce.7.cloned.1.call-update) | async-done | bytes 262160 | tf_op jit(solution)/shard_map/psum | solution.py:32
  346.6 5.3 fusion.32
  351.9 62.0 %collective-permute-done.9 = f32[8,256,256]{1,2,0:T(8,128)} collective-permute-done((f32[8,256,256]{1,2,0:T(8,128)}, f32[8,256,256]{1,2,0:T(8,128)}, u32[]{:S(2)}, u32[]{:S(2)}) %collective-permute-start.9) | collective-permute-done | bytes 2097184 | tf_op jit(solution)/shard_map/ppermute | solution.py:14
  413.9 6.9 subtract_select_fusion.2
  422.9 1.3 fusion.57
  425.8 4.1 collective-permute-done.11
  431.5 46.5 %collective-permute-done.12 = f32[8,256,256]{1,2,0:T(8,128)S(1)} collective-permute-done((f32[8,256,256]{1,2,0:T(8,128)S(1)}, f32[8,256,256]{1,2,0:T(8,128)S(1)}, u32[]{:S(2)}, u32[]{:S(2)}) %collective-permute-start.12) | collective-permute-done | bytes 2097184 | tf_op jit(solution)/shard_map/ppermute | solution.py:14
  478.7 2.6 collective-permute-start.10
  481.4 43.8 %collective-permute-done.13 = f32[8,256,256]{1,2,0:T(8,128)S(1)} collective-permute-done((f32[8,256,256]{1,2,0:T(8,128)S(1)}, f32[8,256,256]{1,2,0:T(8,128)S(1)}, u32[]{:S(2)}, u32[]{:S(2)}) %collective-permute-start.13) | collective-permute-done | bytes 2097184 | tf_op jit(solution)/shard_map/ppermute | solution.py:14
  525.2 1.7 add.275
  526.9 2.0 collective-permute-start.14
  529.2 24.2 %all-reduce.9.cloned.1.call-done = f32[256,256]{1,0:T(8,128)} async-done(((f32[256,256]{1,0:T(8,128)}), f32[256,256]{1,0:T(8,128)}) %all-reduce.9.cloned.1.call-update) | async-done | bytes 262160 | tf_op jit(solution)/shard_map/psum | solution.py:32
  553.4 5.3 fusion.28
  558.7 60.3 %collective-permute-done.14 = f32[8,256,256]{1,2,0:T(8,128)} collective-permute-done((f32[8,256,256]{1,2,0:T(8,128)}, f32[8,256,256]{1,2,0:T(8,128)}, u32[]{:S(2)}, u32[]{:S(2)}) %collective-permute-start.14) | collective-permute-done | bytes 2097184 | tf_op jit(solution)/shard_map/ppermute | solution.py:14
  619.0 6.9 subtract_select_fusion.1
  628.0 1.3 fusion.60
  630.9 4.1 collective-permute-done.16
  636.6 46.5 %collective-permute-done.17 = f32[8,256,256]{1,2,0:T(8,128)S(1)} collective-permute-done((f32[8,256,256]{1,2,0:T(8,128)S(1)}, f32[8,256,256]{1,2,0:T(8,128)S(1)}, u32[]{:S(2)}, u32[]{:S(2)}) %collective-permute-start.17) | collective-permute-done | bytes 2097184 | tf_op jit(solution)/shard_map/ppermute | solution.py:14
  683.9 5.0 collective-permute-start.15
  688.8 41.5 %collective-permute-done.18 = f32[8,256,256]{1,2,0:T(8,128)S(1)} collective-permute-done((f32[8,256,256]{1,2,0:T(8,128)S(1)}, f32[8,256,256]{1,2,0:T(8,128)S(1)}, u32[]{:S(2)}, u32[]{:S(2)}) %collective-permute-start.18) | collective-permute-done | bytes 2097184 | tf_op jit(solution)/shard_map/ppermute | solution.py:14
  730.3 1.6 add.287
  732.0 2.0 collective-permute-start.19
  734.0 24.5 %all-reduce.11.cloned.1.call-done = f32[256,256]{1,0:T(8,128)} async-done(((f32[256,256]{1,0:T(8,128)}), f32[256,256]{1,0:T(8,128)}) %all-reduce.11.cloned.1.call-update) | async-done | bytes 262160 | tf_op jit(solution)/shard_map/psum | solution.py:32
  758.5 5.3 fusion.24
  763.8 60.3 %collective-permute-done.19 = f32[8,256,256]{1,2,0:T(8,128)} collective-permute-done((f32[8,256,256]{1,2,0:T(8,128)}, f32[8,256,256]{1,2,0:T(8,128)}, u32[]{:S(2)}, u32[]{:S(2)}) %collective-permute-start.19) | collective-permute-done | bytes 2097184 | tf_op jit(solution)/shard_map/ppermute | solution.py:14
  824.1 8.2 fusion
  832.3 6.0 copy.27
  (88 shorter events, 29.9 us)
Async XLA Ops:
  6.5 1.7 copy-start
  6.5 5.6 copy-start.9
  6.5 134.9 %all-reduce.5.cloned.1.call-start = ((), (), s32[]{:S(2)}) async-start(), calls=%async_computation | async-start | bytes 524288 | tf_op jit(solution)/shard_map/psum | solution.py:32
  13.6 4.3 collective-permute-start.1
  18.2 51.1 %copy-start.10 = (f32[8,1,256,1,256]{4,3,2,1,0:T(1,128)S(1)}, f32[8,1,256,1,256]{4,3,2,1,0:T(1,128)}, u32[]{:S(2)}) copy-start(f32[8,1,256,1,256]{4,3,2,1,0:T(1,128)} %param.10) | copy-start | bytes 6291460
  18.2 48.8 %collective-permute-start.2 = (f32[8,256,256]{1,2,0:T(8,128)S(1)}, f32[8,256,256]{1,2,0:T(8,128)S(1)}, u32[]{:S(2)}, u32[]{:S(2)}) collective-permute-start(f32[8,256,256]{1,2,0:T(8,128)S(1)} %fusion.17), channel_id=1, source_target_pairs={{0,2},{1,3},{2,0},{3,1},{4,6},{5,7},{6,4},{7,5},{8,10},{9,11},{10,... | collective-permute-start | bytes 6291464 | tf_op jit(solution)/shard_map/ppermute | solution.py:14
  67.4 4.9 copy-start.8
  67.5 47.2 %collective-permute-start.3 = (f32[8,256,256]{1,2,0:T(8,128)S(1)}, f32[8,256,256]{1,2,0:T(8,128)S(1)}, u32[]{:S(2)}, u32[]{:S(2)}) collective-permute-start(f32[8,256,256]{1,2,0:T(8,128)S(1)} %fusion.115), channel_id=1, source_target_pairs={{0,4},{1,5},{2,6},{3,7},{4,0},{5,1},{6,2},{7,3},{8,12},{9,13},{10,... | collective-permute-start | bytes 6291464 | tf_op jit(solution)/shard_map/ppermute | solution.py:14
  70.9 54.4 %collective-permute-start.5 = (f32[8,256,256]{2,1,0:T(8,128)}, f32[8,256,256]{2,1,0:T(8,128)}, u32[]{:S(2)}, u32[]{:S(2)}) collective-permute-start(f32[8,256,256]{2,1,0:T(8,128)} %bitcast.121), channel_id=1, source_target_pairs={{0,16},{16,0},{1,17},{17,1},{2,18},{18,2},{3,19},{19,3},{4,20},{20... | collective-permute-start | bytes 6291464 | tf_op jit(solution)/shard_map/ppermute | solution.py:27
  73.9 67.5 %collective-permute-start = (f32[8,256,256]{2,1,0:T(8,128)}, f32[8,256,256]{2,1,0:T(8,128)}, u32[]{:S(2)}, u32[]{:S(2)}) collective-permute-start(f32[8,256,256]{2,1,0:T(8,128)} %bitcast.122), channel_id=1, source_target_pairs={{1,0},{2,1},{3,2},{4,3},{5,4},{6,5},{7,6},{8,7},{9,8},{10,9},{11,1... | collective-permute-start | bytes 6291464 | tf_op jit(solution)/shard_map/ppermute | solution.py:21
  116.2 92.5 %collective-permute-start.4 = (f32[8,256,256]{1,2,0:T(8,128)}, f32[8,256,256]{1,2,0:T(8,128)}, u32[]{:S(2)}, u32[]{:S(2)}) collective-permute-start(f32[8,256,256]{1,2,0:T(8,128)} %add.252), channel_id=1, source_target_pairs={{0,8},{1,9},{2,10},{3,11},{4,12},{5,13},{6,14},{7,15},{8,0},{9,1},... | collective-permute-start | bytes 6291464 | tf_op jit(solution)/shard_map/ppermute | solution.py:14
  118.8 227.8 %all-reduce.7.cloned.1.call-start = ((), (), s32[]{:S(2)}) async-start(), calls=%async_computation.1 | async-start | bytes 524288 | tf_op jit(solution)/shard_map/psum | solution.py:32
  141.4 67.3 %copy-start.3 = (f32[10,256,256]{2,1,0:T(8,128)S(1)}, f32[10,256,256]{2,1,0:T(8,128)}, u32[]{:S(2)}) copy-start(f32[10,256,256]{2,1,0:T(8,128)} %get-tuple-element.8) | copy-start | bytes 7864324
  208.7 8.7 %copy-start.11 = (f32[1,256,256]{2,1,0:T(8,128)S(1)}, f32[1,256,256]{2,1,0:T(8,128)}, u32[]{:S(2)}) copy-start(f32[1,256,256]{2,1,0:T(8,128)} %param.15) | copy-start | bytes 786436
  208.7 8.7 %copy-start.12 = (f32[1,256]{1,0:T(1,128)S(1)}, f32[1,256]{1,0:T(1,128)}, u32[]{:S(2)}) copy-start(f32[1,256]{1,0:T(1,128)} %param.17) | copy-start | bytes 3076
  215.6 1.3 copy-start.6
  220.6 4.2 collective-permute-start.6
  225.1 47.7 %collective-permute-start.7 = (f32[8,256,256]{1,2,0:T(8,128)S(1)}, f32[8,256,256]{1,2,0:T(8,128)S(1)}, u32[]{:S(2)}, u32[]{:S(2)}) collective-permute-start(f32[8,256,256]{1,2,0:T(8,128)S(1)} %fusion.18), channel_id=1, source_target_pairs={{0,2},{1,3},{2,0},{3,1},{4,6},{5,7},{6,4},{7,5},{8,10},{9,11},{10,... | collective-permute-start | bytes 6291464 | tf_op jit(solution)/shard_map/ppermute | solution.py:14
  273.2 46.9 %collective-permute-start.8 = (f32[8,256,256]{1,2,0:T(8,128)S(1)}, f32[8,256,256]{1,2,0:T(8,128)S(1)}, u32[]{:S(2)}, u32[]{:S(2)}) collective-permute-start(f32[8,256,256]{1,2,0:T(8,128)S(1)} %fusion.114), channel_id=1, source_target_pairs={{0,4},{1,5},{2,6},{3,7},{4,0},{5,1},{6,2},{7,3},{8,12},{9,13},{10,... | collective-permute-start | bytes 6291464 | tf_op jit(solution)/shard_map/ppermute | solution.py:14
  321.8 92.1 %collective-permute-start.9 = (f32[8,256,256]{1,2,0:T(8,128)}, f32[8,256,256]{1,2,0:T(8,128)}, u32[]{:S(2)}, u32[]{:S(2)}) collective-permute-start(f32[8,256,256]{1,2,0:T(8,128)} %add.264), channel_id=1, source_target_pairs={{0,8},{1,9},{2,10},{3,11},{4,12},{5,13},{6,14},{7,15},{8,0},{9,1},... | collective-permute-start | bytes 6291464 | tf_op jit(solution)/shard_map/ppermute | solution.py:14
  323.8 229.6 %all-reduce.9.cloned.1.call-start = ((), (), s32[]{:S(2)}) async-start(), calls=%async_computation.2 | async-start | bytes 524288 | tf_op jit(solution)/shard_map/psum | solution.py:32
  346.6 67.3 %copy-start.1 = (f32[10,256,256]{2,1,0:T(8,128)S(1)}, f32[10,256,256]{2,1,0:T(8,128)}, u32[]{:S(2)}) copy-start(f32[10,256,256]{2,1,0:T(8,128)} %get-tuple-element.7) | copy-start | bytes 7864324
  420.8 1.3 copy-start.5
  425.7 4.2 collective-permute-start.11
  430.2 47.7 %collective-permute-start.12 = (f32[8,256,256]{1,2,0:T(8,128)S(1)}, f32[8,256,256]{1,2,0:T(8,128)S(1)}, u32[]{:S(2)}, u32[]{:S(2)}) collective-permute-start(f32[8,256,256]{1,2,0:T(8,128)S(1)} %fusion.19), channel_id=1, source_target_pairs={{0,2},{1,3},{2,0},{3,1},{4,6},{5,7},{6,4},{7,5},{8,10},{9,11},{10,... | collective-permute-start | bytes 6291464 | tf_op jit(solution)/shard_map/ppermute | solution.py:14
  478.3 46.9 %collective-permute-start.13 = (f32[8,256,256]{1,2,0:T(8,128)S(1)}, f32[8,256,256]{1,2,0:T(8,128)S(1)}, u32[]{:S(2)}, u32[]{:S(2)}) collective-permute-start(f32[8,256,256]{1,2,0:T(8,128)S(1)} %fusion.113), channel_id=1, source_target_pairs={{0,4},{1,5},{2,6},{3,7},{4,0},{5,1},{6,2},{7,3},{8,12},{9,13},{10,... | collective-permute-start | bytes 6291464 | tf_op jit(solution)/shard_map/ppermute | solution.py:14
  478.7 50.4 %collective-permute-start.10 = (f32[8,256,256]{2,1,0:T(8,128)}, f32[8,256,256]{2,1,0:T(8,128)}, u32[]{:S(2)}, u32[]{:S(2)}) collective-permute-start(f32[8,256,256]{2,1,0:T(8,128)} %bitcast.122), channel_id=1, source_target_pairs={{0,1},{1,2},{2,3},{3,4},{4,5},{5,6},{6,7},{7,8},{8,9},{9,10},{10,1... | collective-permute-start | bytes 6291464 | tf_op jit(solution)/shard_map/ppermute | solution.py:21
  526.9 92.1 %collective-permute-start.14 = (f32[8,256,256]{1,2,0:T(8,128)}, f32[8,256,256]{1,2,0:T(8,128)}, u32[]{:S(2)}, u32[]{:S(2)}) collective-permute-start(f32[8,256,256]{1,2,0:T(8,128)} %add.275), channel_id=1, source_target_pairs={{0,8},{1,9},{2,10},{3,11},{4,12},{5,13},{6,14},{7,15},{8,0},{9,1},... | collective-permute-start | bytes 6291464 | tf_op jit(solution)/shard_map/ppermute | solution.py:14
  528.9 229.6 %all-reduce.11.cloned.1.call-start = ((), (), s32[]{:S(2)}) async-start(), calls=%async_computation.3 | async-start | bytes 524288 | tf_op jit(solution)/shard_map/psum | solution.py:32
  553.4 65.6 %copy-start.4 = (f32[10,256,256]{2,1,0:T(8,128)S(1)}, f32[10,256,256]{2,1,0:T(8,128)}, u32[]{:S(2)}) copy-start(f32[10,256,256]{2,1,0:T(8,128)} %get-tuple-element.8) | copy-start | bytes 7864324
  625.9 1.3 copy-start.7
  630.8 4.2 collective-permute-start.16
  635.4 47.7 %collective-permute-start.17 = (f32[8,256,256]{1,2,0:T(8,128)S(1)}, f32[8,256,256]{1,2,0:T(8,128)S(1)}, u32[]{:S(2)}, u32[]{:S(2)}) collective-permute-start(f32[8,256,256]{1,2,0:T(8,128)S(1)} %fusion.20), channel_id=1, source_target_pairs={{0,2},{1,3},{2,0},{3,1},{4,6},{5,7},{6,4},{7,5},{8,10},{9,11},{10,... | collective-permute-start | bytes 6291464 | tf_op jit(solution)/shard_map/ppermute | solution.py:14
  683.5 46.9 %collective-permute-start.18 = (f32[8,256,256]{1,2,0:T(8,128)S(1)}, f32[8,256,256]{1,2,0:T(8,128)S(1)}, u32[]{:S(2)}, u32[]{:S(2)}) collective-permute-start(f32[8,256,256]{1,2,0:T(8,128)S(1)} %fusion.112), channel_id=1, source_target_pairs={{0,4},{1,5},{2,6},{3,7},{4,0},{5,1},{6,2},{7,3},{8,12},{9,13},{10,... | collective-permute-start | bytes 6291464 | tf_op jit(solution)/shard_map/ppermute | solution.py:14
  683.9 50.1 %collective-permute-start.15 = (f32[8,256,256]{2,1,0:T(8,128)}, f32[8,256,256]{2,1,0:T(8,128)}, u32[]{:S(2)}, u32[]{:S(2)}) collective-permute-start(f32[8,256,256]{2,1,0:T(8,128)} %bitcast.122), channel_id=1, source_target_pairs={{0,2},{1,3},{2,4},{3,5},{4,6},{5,7},{6,8},{7,9},{8,10},{9,11},{10,... | collective-permute-start | bytes 6291464 | tf_op jit(solution)/shard_map/ppermute | solution.py:21
  732.0 92.1 %collective-permute-start.19 = (f32[8,256,256]{1,2,0:T(8,128)}, f32[8,256,256]{1,2,0:T(8,128)}, u32[]{:S(2)}, u32[]{:S(2)}) collective-permute-start(f32[8,256,256]{1,2,0:T(8,128)} %add.287), channel_id=1, source_target_pairs={{0,8},{1,9},{2,10},{3,11},{4,12},{5,13},{6,14},{7,15},{8,0},{9,1},... | collective-permute-start | bytes 6291464 | tf_op jit(solution)/shard_map/ppermute | solution.py:14
  758.5 65.6 %copy-start.2 = (f32[10,256,256]{2,1,0:T(8,128)S(1)}, f32[10,256,256]{2,1,0:T(8,128)}, u32[]{:S(2)}) copy-start(f32[10,256,256]{2,1,0:T(8,128)} %get-tuple-element.7) | copy-start | bytes 7864324
Sparse Core Ops, SparseCore 0:
  118.9 22.5 all-reduce.4
  323.9 22.6 all-reduce.6
  529.0 24.3 all-reduce.8
  734.1 24.3 all-reduce.10
